TPU v7x, 32 devices: a whole 2x2x4 slice. The times are simulated.
32 devices in a mesh: row: 8 (over y, x, core), col: 4 (over z).
Axes of the slice: x: 2, y: 2, z: 4, core: 2. Of those that a mesh axis runs over, the one named last changes fastest.
Arguments:
- temps: bfloat16 [12, 64, 16384], P(None, None, ('row', 'col')), may hold values from -6 to 6
- sensors: int32 [12, 512], replicated, may hold values from 0 to 16383
Outputs:
- corr: bfloat16 [512, 16384], P('col', 'row')
Inputs may be any that keep to these rules, and one draw needn't show every extreme that they name: `sensors`: each entry is a pixel index of its tier; candidates may repeat.
All inputs are finite; a program needn't handle non-finite values.
Results may differ from a plain program's by a relative error of at most 0.001.
Values may be sent and summed in bfloat16 or wider, within the bound.
A program may use at most 64 MiB of HBM per device.

v0:
```python
import functools

import jax
import numpy as np
import jax.numpy as jnp
from jax import lax
from jax.experimental import pallas as pl
from jax.experimental.pallas import tpu as pltpu
from jax.sharding import PartitionSpec as P

SUB = 16
MESH = pl.DeviceIdType.MESH


def kernel(
    n_row, n_col, n_chunk, tiers,
    temps_hbm, sens_ref, out_ref,
    temps_ref, sens_t, part, core_buf, pair_sum, rs_buf, z_src, z_buf, full, out_buf,
    c_send, c_recv, rs_send, rs_recv, z_send, z_recv,
    ag_send, ag_recv, d_send, d_recv, o_send, o_recv, t_sem,
):
    r = lax.axis_index("row")
    z = lax.axis_index("col")
    core, chip = lax.rem(r, 2), r // 2
    other = 1 - core
    n_chip = n_row // 2
    snaps, width = temps_ref.shape[0] // tiers, temps_ref.shape[1]
    depth = temps_ref.shape[0]
    rows_col = out_ref.shape[0] // n_chunk
    half = rows_col // 2
    rows_half = n_chip * SUB
    scale = float(np.float32(1.0) / np.sqrt(np.float32(depth)))
    partner = (chip * 2 + other, z)

    def chip_peer(d):
        peer = lax.rem(chip + d, n_chip)
        return peer, (peer * 2 + core, z)

    n_half = n_col // 2
    side = z // n_half

    def col_peer(e):
        return lax.rem(z + e, n_col)

    def out_peer(e):
        across = (1 - side) * n_half + lax.rem(z + e, n_half)
        beside = side * n_half + lax.rem(z + e, n_half)
        return across if e < n_half else beside

    load = pltpu.make_async_copy(temps_hbm, temps_ref, t_sem)
    load.start()
    barrier = pltpu.get_barrier_semaphore()
    pl.semaphore_signal(barrier, inc=1, device_id=partner, device_id_type=MESH)
    for d in range(1, n_chip):
        pl.semaphore_signal(barrier, inc=1, device_id=chip_peer(d)[1], device_id_type=MESH)
    for e in range(1, n_col):
        pl.semaphore_signal(barrier, inc=1, device_id=(r, col_peer(e)), device_id_type=MESH)

    first_pixel = (r * n_col + z) * width
    offsets = jnp.transpose(sens_ref[...] - first_pixel)
    sens_t[...] = offsets.reshape(sens_t.shape)
    pixel_ids = lax.broadcasted_iota(jnp.int32, (rows_half, width), 1)

    def wait_all(ref, sem):
        pltpu.make_async_copy(ref, ref, sem).wait()

    def select(k):
        for h in range(2):
            mine = sens_t[:, k, h].reshape(rows_half, tiers)
            for t in range(0, tiers, 2):
                pair = []
                for u in (t, t + 1):
                    hot = (pixel_ids == mine[:, u:u + 1]).astype(jnp.float32).astype(jnp.bfloat16)
                    pair.append(lax.dot_general(
                        hot, temps_ref[u * snaps:(u + 1) * snaps, :],
                        (((1,), (1,)), ((), ())), preferred_element_type=jnp.float32,
                    ))
                both = jnp.concatenate(pair, axis=1).astype(jnp.bfloat16)
                part[k, h, :, :, t * snaps:(t + 2) * snaps] = both.reshape(n_chip, SUB, 2 * snaps)

    def start_core(k):
        pltpu.make_async_remote_copy(
            part.at[k, other], core_buf.at[k], c_send.at[k], c_recv.at[k],
            device_id=partner, device_id_type=MESH,
        ).start()

    def start_rs(k):
        wait_all(core_buf.at[k], c_recv.at[k])
        pair_sum[k] = part[k, core] + core_buf[k]
        for d in range(1, n_chip):
            peer, device = chip_peer(d)
            pltpu.make_async_remote_copy(
                pair_sum.at[k, peer], rs_buf.at[k, d - 1], rs_send.at[k], rs_recv.at[k],
                device_id=device, device_id_type=MESH,
            ).start()

    def start_z(k):
        wait_all(rs_buf.at[k], rs_recv.at[k])
        total = pair_sum[k, chip]
        for d in range(n_chip - 1):
            total = total + rs_buf[k, d]
        z_src[k] = total
        for e in range(1, n_col):
            pltpu.make_async_remote_copy(
                z_src.at[k], z_buf.at[k, e - 1], z_send.at[k], z_recv.at[k],
                device_id=(r, col_peer(e)), device_id_type=MESH,
            ).start()

    def start_ag(k):
        wait_all(z_buf.at[k], z_recv.at[k])
        total = z_src[k]
        for e in range(n_col - 1):
            total = total + z_buf[k, e]
        full[k, core, chip] = total
        for d in range(1, n_chip):
            pltpu.make_async_remote_copy(
                full.at[k, core, chip], full.at[k, core, chip], ag_send.at[k], ag_recv.at[k],
                device_id=chip_peer(d)[1], device_id_type=MESH,
            ).start()

    def start_pass(k):
        wait_all(rs_buf.at[k], ag_recv.at[k])
        pltpu.make_async_remote_copy(
            full.at[k, core], full.at[k, core], d_send.at[k], d_recv.at[k],
            device_id=partner, device_id_type=MESH,
        ).start()

    def start_out(k):
        wait_all(core_buf.at[k], d_recv.at[k])
        readings = full[k].reshape(2 * rows_half, depth)
        summed = jnp.dot(readings, temps_ref[...], preferred_element_type=jnp.float32)
        rounded = (summed * scale).astype(jnp.bfloat16)
        for h in range(2):
            out_buf[k, :, h * half:(h + 1) * half] = rounded[h * rows_half:(h + 1) * rows_half].reshape(n_col, half, width)
        rows = pl.ds(k * rows_col, rows_col)
        columns = pl.ds(pl.multiple_of(z * width, width), width)
        for e in [*range(n_half), *range(n_half + 1, n_col)]:
            peer = out_peer(e)
            pltpu.make_async_remote_copy(
                out_buf.at[k, peer], out_ref.at[rows, columns], o_send.at[k], o_recv.at[k],
                device_id=(r, peer), device_id_type=MESH,
            ).start()
        out_ref[rows, columns] = out_buf[k, z]

    load.wait()
    select(0)
    pl.semaphore_wait(barrier, n_chip + n_col - 1)
    start_core(0)
    for k in range(1, n_chunk):
        select(k)
        start_core(k)
        start_rs(k - 1)
    start_rs(n_chunk - 1)
    stages = (start_z, start_ag, start_pass, start_out)
    due = [(at + 3.0 * k, late, k) for late, at in enumerate((0, 4.5, 8, 9.2)) for k in range(n_chunk)]
    for _, late, k in sorted(due):
        stages[late](k)
    for k in range(n_chunk):
        wait_all(out_buf.at[k, pl.ds(0, n_col - 1)], o_recv.at[k])
        wait_all(core_buf.at[k], c_send.at[k])
        wait_all(rs_buf.at[k], rs_send.at[k])
        wait_all(z_buf.at[k], z_send.at[k])
        wait_all(rs_buf.at[k], ag_send.at[k])
        wait_all(core_buf.at[k], d_send.at[k])
        wait_all(out_buf.at[k, pl.ds(0, n_col - 1)], o_send.at[k])


def body(n_row, n_col, temps, sensors):
    tiers, snaps, width = temps.shape
    sens = sensors.shape[1]
    depth = tiers * snaps
    n_chunk = sens // (SUB * n_row)
    n_chip = n_row // 2
    rows_out = sens // n_col
    rows_col = rows_out // n_chunk
    bf16 = jnp.bfloat16
    return pl.pallas_call(
        functools.partial(kernel, n_row, n_col, n_chunk, tiers),
        out_shape=pltpu.VMEM((rows_out, n_col * width), bf16),
        in_specs=[pl.BlockSpec(memory_space=pl.ANY), pl.BlockSpec(memory_space=pltpu.VMEM)],
        out_specs=pl.BlockSpec(memory_space=pltpu.VMEM),
        scratch_shapes=[
            pltpu.VMEM((depth, width), bf16),
            pltpu.VMEM((n_col, n_chunk, 2, rows_col // 2, tiers), jnp.int32),
            pltpu.VMEM((n_chunk, 2, n_chip, SUB, depth), bf16),
            pltpu.VMEM((n_chunk, n_chip, SUB, depth), bf16),
            pltpu.VMEM((n_chunk, n_chip, SUB, depth), bf16),
            pltpu.VMEM((n_chunk, n_chip - 1, SUB, depth), bf16),
            pltpu.VMEM((n_chunk, SUB, depth), bf16),
            pltpu.VMEM((n_chunk, n_col - 1, SUB, depth), bf16),
            pltpu.VMEM((n_chunk, 2, n_chip, SUB, depth), bf16),
            pltpu.VMEM((n_chunk, n_col, rows_col, width), bf16),
        ] + [pltpu.SemaphoreType.DMA((n_chunk,))] * 12 + [pltpu.SemaphoreType.DMA],
        compiler_params=pltpu.CompilerParams(collective_id=0, has_side_effects=True),
    )(temps.reshape(depth, width), sensors)


def solution(mesh):
    placed = (P(None, None, ("row", "col")), P())
    return jax.shard_map(
        functools.partial(body, mesh.shape["row"], mesh.shape["col"]),
        mesh=mesh, in_specs=placed, out_specs=P("col", "row"), check_vma=False,
    )
```

profile of v0, /device:TPU:0, one launch (start us, length us, event | category | flops | bytes accessed | tf_op | source)
XLA Modules:
  0.0 33.9 jit_solution(398406487779118889)
XLA Ops:
  0.0 33.1 %shard_map.28 = bf16[128,2048]{1,0:T(8,128)(2,1)S(1)} custom-call(bf16[768,512]{1,0:T(8,128)(2,1)} %bitcast.1, s32[12,512]{1,0:T(8,128)} %sens_ref.1), custom_call_target="tpu_custom_call" | custom-call | tf_op jit(solution)/shard_map/pallas_call | solution.py:177
  33.1 0.8 %copy.4 = bf16[128,2048]{1,0:T(8,128)(2,1)} copy(bf16[128,2048]{1,0:T(8,128)(2,1)S(1)} %shard_map.28) | data formatting | bytes 1048576
where the time goes:
time: 34.3 us; the launch traced here: 33.9 us
  Pallas kernels  33.1 us (97%)
  local copies, waits for them, and re-layouts  0.8 us (2%)
    pallas_call x1, Pallas kernels, body(): pl.pallas_call(functools.partial(kernel, n_row, n_col, n_chunk, tiers), o...  33.1 us
    unnamed x1, local copies, waits for them, and re-layouts  0.8 us

commit v1 on v0

v1 whole, which is shorter than its diff:
```python
import functools

import jax
import numpy as np
import jax.numpy as jnp
from jax import lax
from jax.experimental import pallas as pl
from jax.experimental.pallas import tpu as pltpu
from jax.sharding import PartitionSpec as P

SUB = 16
MESH = pl.DeviceIdType.MESH


def kernel(
    n_row, n_col, n_chunk, tiers,
    temps_hbm, sens_ref, out_ref,
    temps_ref, sens_t, part, core_buf, pair_sum, rs_buf, z_src, z_buf, full, out_buf,
    c_send, c_recv, rs_send, rs_recv, z_send, z_recv,
    ag_send, ag_recv, o_send, o_recv, t_sem, x_send, x_recv,
):
    r = lax.axis_index("row")
    z = lax.axis_index("col")
    core, chip = lax.rem(r, 2), r // 2
    other = 1 - core
    pair, parity = z // 2, lax.rem(z, 2)
    n_chip, n_pair = n_row // 2, n_col // 2
    depth, width = temps_ref.shape[1:]
    snaps, deep = depth // tiers, depth // 2
    rows_col = out_ref.shape[0] // n_chunk
    half = rows_col // 2
    rows_half = n_chip * SUB
    scale = float(np.float32(1.0) / np.sqrt(np.float32(depth)))
    partner = (chip * 2 + other, z)

    cube = [(d, e) for d in reversed(range(n_chip)) for e in (1, 0) if d or e]

    def cube_peer(d, e):
        peer = lax.rem(chip + d, n_chip)
        side = lax.rem(parity + e, 2)
        return side, peer, (peer * 2 + core, pair * 2 + side)

    def far_peer(e):
        return lax.rem(z + 2 * e, n_col)

    def column_peer(h, e):
        return (chip * 2 + lax.rem(core + h, 2), lax.rem(z + e, n_col))

    load = pltpu.make_async_copy(temps_hbm, temps_ref.at[core], t_sem)
    load.start()
    barrier = pltpu.get_barrier_semaphore()
    greeted = 0
    for d, e in cube:
        if d:
            pl.semaphore_signal(barrier, inc=1, device_id=cube_peer(d, e)[2], device_id_type=MESH)
            greeted += 1
    for h in range(2):
        for e in range(n_col):
            if h or e:
                pl.semaphore_signal(barrier, inc=1, device_id=column_peer(h, e), device_id_type=MESH)
                greeted += 1

    first_pixel = (r * n_col + z) * width
    offsets = jnp.transpose(sens_ref[...] - first_pixel)
    sens_t[...] = offsets.reshape(sens_t.shape)
    pixel_ids = lax.broadcasted_iota(jnp.int32, (rows_half, width), 1)

    def wait_all(ref, sem):
        pltpu.make_async_copy(ref, ref, sem).wait()

    def select(k):
        for h in range(2):
            mine = sens_t[:, k, h].reshape(rows_half, tiers)
            for t in range(0, tiers, 2):
                two = []
                for u in (t, t + 1):
                    hot = (pixel_ids == mine[:, u:u + 1]).astype(jnp.float32).astype(jnp.bfloat16)
                    two.append(lax.dot_general(
                        hot, temps_ref[core, u * snaps:(u + 1) * snaps, :],
                        (((1,), (1,)), ((), ())), preferred_element_type=jnp.float32,
                    ))
                both = jnp.concatenate(two, axis=1).astype(jnp.bfloat16)
                b, at = divmod(t * snaps, deep)
                part[k, h, b, :, :, at:at + 2 * snaps] = both.reshape(n_chip, SUB, 2 * snaps)

    def start_core(k):
        pltpu.make_async_remote_copy(
            part.at[k, other], core_buf.at[k], c_send.at[k], c_recv.at[k],
            device_id=partner, device_id_type=MESH,
        ).start()

    def start_rs(k):
        wait_all(core_buf.at[k], c_recv.at[k])
        pair_sum[k] = part[k, core] + core_buf[k]
        for slot, (d, e) in enumerate(cube):
            side, peer, device = cube_peer(d, e)
            pltpu.make_async_remote_copy(
                pair_sum.at[k, side, peer], rs_buf.at[k, slot], rs_send.at[k], rs_recv.at[k],
                device_id=device, device_id_type=MESH,
            ).start()

    def start_z(k):
        wait_all(rs_buf.at[k], rs_recv.at[k])
        total = pair_sum[k, parity, chip]
        for slot in range(len(cube)):
            total = total + rs_buf[k, slot]
        z_src[k] = total
        for e in range(1, n_pair):
            pltpu.make_async_remote_copy(
                z_src.at[k], z_buf.at[k, e - 1], z_send.at[k], z_recv.at[k],
                device_id=(r, far_peer(e)), device_id_type=MESH,
            ).start()

    def start_ag(k):
        wait_all(z_buf.at[k], z_recv.at[k])
        total = z_src[k]
        for e in range(n_pair - 1):
            total = total + z_buf[k, e]
        full[k, parity, chip] = total
        for d, e in cube:
            pltpu.make_async_remote_copy(
                full.at[k, parity, chip], full.at[k, parity, chip], ag_send.at[k], ag_recv.at[k],
                device_id=cube_peer(d, e)[2], device_id_type=MESH,
            ).start()

    n_half = n_col // 2
    side_z = z // n_half

    def out_peer(e):
        across = (1 - side_z) * n_half + lax.rem(z + e, n_half)
        beside = side_z * n_half + lax.rem(z + e, n_half)
        return across if e < n_half else beside

    def start_out(k):
        if k == 0:
            wait_all(temps_ref.at[other], x_recv)
        wait_all(rs_buf.at[k], ag_recv.at[k])
        rows = pl.ds(pl.multiple_of(k * rows_col + core * half, half), half)
        columns = pl.ds(pl.multiple_of(z * width, width), width)
        readings = [full[k, b].reshape(rows_half, deep) for b in range(2)]
        for h in range(2):
            summed = jnp.dot(readings[0], temps_ref[h, :deep, :], preferred_element_type=jnp.float32)
            summed += jnp.dot(readings[1], temps_ref[h, deep:, :], preferred_element_type=jnp.float32)
            rounded = (summed * scale).astype(jnp.bfloat16)
            out_buf[k, h * n_col:(h + 1) * n_col] = rounded.reshape(n_col, half, width)
            for e in [*range(n_half), *range(n_half + 1, n_col)]:
                peer = out_peer(e)
                pltpu.make_async_remote_copy(
                    out_buf.at[k, h * n_col + peer], out_ref.at[rows, columns], o_send.at[k], o_recv.at[k],
                    device_id=(chip * 2 + h, peer), device_id_type=MESH,
                ).start()
        pltpu.make_async_remote_copy(
            out_buf.at[k, other * n_col + z], out_ref.at[rows, columns], o_send.at[k], o_recv.at[k],
            device_id=partner, device_id_type=MESH,
        ).start()
        out_ref[rows, columns] = out_buf[k, core * n_col + z]

    load.wait()
    select(0)
    pl.semaphore_wait(barrier, greeted)
    start_core(0)
    for k in range(1, n_chunk):
        select(k)
        start_core(k)
        start_rs(k - 1)
    pltpu.make_async_remote_copy(
        temps_ref.at[core], temps_ref.at[core], x_send, x_recv,
        device_id=partner, device_id_type=MESH,
    ).start()
    start_rs(n_chunk - 1)
    stages = (start_z, start_ag, start_out)
    due = [(at + 1.05 * k, late, k) for late, at in enumerate((0, 2.7, 6.5)) for k in range(n_chunk)]
    for _, late, k in sorted(due):
        stages[late](k)
    wait_all(temps_ref.at[core], x_send)
    for k in range(n_chunk):
        wait_all(out_buf.at[k, pl.ds(0, 2 * n_col - 1)], o_recv.at[k])
        wait_all(out_buf.at[k, pl.ds(0, 2 * n_col - 1)], o_send.at[k])
        wait_all(core_buf.at[k], c_send.at[k])
        wait_all(rs_buf.at[k], rs_send.at[k])
        wait_all(z_buf.at[k], z_send.at[k])
        wait_all(rs_buf.at[k], ag_send.at[k])


def body(n_row, n_col, temps, sensors):
    tiers, snaps, width = temps.shape
    sens = sensors.shape[1]
    depth = tiers * snaps
    n_chunk = sens // (SUB * n_row)
    n_chip = n_row // 2
    rows_out = sens // n_col
    rows_col = rows_out // n_chunk
    bf16 = jnp.bfloat16
    return pl.pallas_call(
        functools.partial(kernel, n_row, n_col, n_chunk, tiers),
        out_shape=pltpu.VMEM((rows_out, n_col * width), bf16),
        in_specs=[pl.BlockSpec(memory_space=pl.ANY), pl.BlockSpec(memory_space=pltpu.VMEM)],
        out_specs=pl.BlockSpec(memory_space=pltpu.VMEM),
        scratch_shapes=[
            pltpu.VMEM((2, depth, width), bf16),
            pltpu.VMEM((n_col, n_chunk, 2, rows_col // 2, tiers), jnp.int32),
            pltpu.VMEM((n_chunk, 2, 2, n_chip, SUB, depth // 2), bf16),
            pltpu.VMEM((n_chunk, 2, n_chip, SUB, depth // 2), bf16),
            pltpu.VMEM((n_chunk, 2, n_chip, SUB, depth // 2), bf16),
            pltpu.VMEM((n_chunk, 2 * n_chip - 1, SUB, depth // 2), bf16),
            pltpu.VMEM((n_chunk, SUB, depth // 2), bf16),
            pltpu.VMEM((n_chunk, n_col // 2 - 1, SUB, depth // 2), bf16),
            pltpu.VMEM((n_chunk, 2, n_chip, SUB, depth // 2), bf16),
            pltpu.VMEM((n_chunk, 2 * n_col, rows_col // 2, width), bf16),
        ] + [pltpu.SemaphoreType.DMA((n_chunk,))] * 10 + [pltpu.SemaphoreType.DMA] * 3,
        compiler_params=pltpu.CompilerParams(collective_id=0, has_side_effects=True),
    )(temps.reshape(depth, width), sensors)


def solution(mesh):
    placed = (P(None, None, ("row", "col")), P())
    return jax.shard_map(
        functools.partial(body, mesh.shape["row"], mesh.shape["col"]),
        mesh=mesh, in_specs=placed, out_specs=P("col", "row"), check_vma=False,
    )
```

time: 34.3 us -> 31.9 us (0.930)
  Pallas kernels: 33.1 us -> 30.9 us
    pallas_call x1, Pallas kernels: 33.1 us -> 30.9 us  [body(): pl.pallas_call(functools.partial(kernel, n_row, n_col, n_chunk, tiers), o...]
where the time goes in v1:
time: 31.9 us; the launch traced here: 31.7 us
  Pallas kernels  30.9 us (97%)
  local copies, waits for them, and re-layouts  0.8 us (3%)
    pallas_call x1, Pallas kernels, body(): pl.pallas_call(functools.partial(kernel, n_row, n_col, n_chunk, tiers), o...  30.9 us
    unnamed x1, local copies, waits for them, and re-layouts  0.8 us

profile of v1, /device:TPU:0, one launch (start us, length us, event | category | flops | bytes accessed | tf_op | source)
XLA Modules:
  0.0 31.7 jit_solution(11816829354473448580)
XLA Ops:
  0.0 30.9 %shard_map.28 = bf16[128,2048]{1,0:T(8,128)(2,1)S(1)} custom-call(bf16[768,512]{1,0:T(8,128)(2,1)} %bitcast.1, s32[12,512]{1,0:T(8,128)} %sens_ref.1), custom_call_target="tpu_custom_call" | custom-call | tf_op jit(solution)/shard_map/pallas_call | solution.py:194
  30.9 0.8 %copy.4 = bf16[128,2048]{1,0:T(8,128)(2,1)} copy(bf16[128,2048]{1,0:T(8,128)(2,1)S(1)} %shard_map.28) | data formatting | bytes 1048576

commit v2 on v1

--- a/solution.py
+++ b/solution.py
@@ -14,10 +14,10 @@
 
 def kernel(
     n_row, n_col, n_chunk, tiers,
-    temps_hbm, sens_ref, out_ref,
-    temps_ref, sens_t, part, core_buf, pair_sum, rs_buf, z_src, z_buf, full, out_buf,
+    temps_hbm, sens_hbm, out_ref,
+    temps_ref, sens_ref, sens_t, part, core_buf, pair_sum, rs_buf, z_src, z_buf, full, out_buf,
     c_send, c_recv, rs_send, rs_recv, z_send, z_recv,
-    ag_send, ag_recv, o_send, o_recv, t_sem, x_send, x_recv,
+    ag_send, ag_recv, o_send, o_recv, t_sem, s_sem, x_send, x_recv, near,
 ):
     r = lax.axis_index("row")
     z = lax.axis_index("col")
@@ -33,55 +33,74 @@
     scale = float(np.float32(1.0) / np.sqrt(np.float32(depth)))
     partner = (chip * 2 + other, z)
 
-    cube = [(d, e) for d in reversed(range(n_chip)) for e in (1, 0) if d or e]
+    bits = n_chip.bit_length() - 1
+    levels = max(bits + 1, n_col - 2)
+    cube = sorted(
+        ((d, e) for d in range(n_chip) for e in range(2) if d or e),
+        key=lambda peer: -peer[0].bit_count() - peer[1],
+    )
+
+    def flip(value, mask):
+        for bit in range(bits):
+            if mask >> bit & 1:
+                value = value + (1 << bit) * (1 - 2 * lax.rem(value // (1 << bit), 2))
+        return value
 
     def cube_peer(d, e):
-        peer = lax.rem(chip + d, n_chip)
+        peer = flip(chip, d)
         side = lax.rem(parity + e, 2)
         return side, peer, (peer * 2 + core, pair * 2 + side)
 
     def far_peer(e):
         return lax.rem(z + 2 * e, n_col)
 
-    def column_peer(h, e):
-        return (chip * 2 + lax.rem(core + h, 2), lax.rem(z + e, n_col))
-
     load = pltpu.make_async_copy(temps_hbm, temps_ref.at[core], t_sem)
+    load_sens = pltpu.make_async_copy(sens_hbm, sens_ref, s_sem)
+    barrier = pltpu.get_barrier_semaphore()
+
+    def greet(sem):
+        pl.semaphore_signal(sem, inc=1, device_id=partner, device_id_type=MESH)
+        for bit in range(bits):
+            pl.semaphore_signal(sem, inc=1, device_id=(flip(chip, 1 << bit) * 2 + core, z), device_id_type=MESH)
+
+        @pl.when(z > 0)
+        def _():
+            pl.semaphore_signal(sem, inc=1, device_id=(r, z - 1), device_id_type=MESH)
+
+        @pl.when(z < n_col - 1)
+        def _():
+            pl.semaphore_signal(sem, inc=1, device_id=(r, z + 1), device_id_type=MESH)
+
+    neighbours = bits + 1 + (z > 0).astype(jnp.int32) + (z < n_col - 1).astype(jnp.int32)
+
+    load_sens.start()
     load.start()
-    barrier = pltpu.get_barrier_semaphore()
-    greeted = 0
-    for d, e in cube:
-        if d:
-            pl.semaphore_signal(barrier, inc=1, device_id=cube_peer(d, e)[2], device_id_type=MESH)
-            greeted += 1
-    for h in range(2):
-        for e in range(n_col):
-            if h or e:
-                pl.semaphore_signal(barrier, inc=1, device_id=column_peer(h, e), device_id_type=MESH)
-                greeted += 1
+    greet(barrier)
 
     first_pixel = (r * n_col + z) * width
-    offsets = jnp.transpose(sens_ref[...] - first_pixel)
-    sens_t[...] = offsets.reshape(sens_t.shape)
-    pixel_ids = lax.broadcasted_iota(jnp.int32, (rows_half, width), 1)
+    load_sens.wait()
+    offsets = jnp.transpose(sens_ref[...] - first_pixel).reshape(n_col, n_chunk, 2, half, tiers)
+    for k in range(n_chunk):
+        for h in range(2):
+            sens_t[k, h] = offsets[:, k, h]
+    pixel_ids = lax.broadcasted_iota(jnp.int32, (2 * rows_half, width), 1)
 
     def wait_all(ref, sem):
         pltpu.make_async_copy(ref, ref, sem).wait()
 
     def select(k):
-        for h in range(2):
-            mine = sens_t[:, k, h].reshape(rows_half, tiers)
-            for t in range(0, tiers, 2):
-                two = []
-                for u in (t, t + 1):
-                    hot = (pixel_ids == mine[:, u:u + 1]).astype(jnp.float32).astype(jnp.bfloat16)
-                    two.append(lax.dot_general(
-                        hot, temps_ref[core, u * snaps:(u + 1) * snaps, :],
-                        (((1,), (1,)), ((), ())), preferred_element_type=jnp.float32,
-                    ))
-                both = jnp.concatenate(two, axis=1).astype(jnp.bfloat16)
-                b, at = divmod(t * snaps, deep)
-                part[k, h, b, :, :, at:at + 2 * snaps] = both.reshape(n_chip, SUB, 2 * snaps)
+        mine = sens_t[k].reshape(2 * rows_half, tiers)
+        for t in range(0, tiers, 2):
+            two = []
+            for u in (t, t + 1):
+                hot = (pixel_ids == mine[:, u:u + 1]).astype(jnp.float32).astype(jnp.bfloat16)
+                two.append(lax.dot_general(
+                    hot, temps_ref[core, u * snaps:(u + 1) * snaps, :],
+                    (((1,), (1,)), ((), ())), preferred_element_type=jnp.float32,
+                ))
+            both = jnp.concatenate(two, axis=1).astype(jnp.bfloat16)
+            b, at = divmod(t * snaps, deep)
+            part[k, :, b, :, :, at:at + 2 * snaps] = both.reshape(2, n_chip, SUB, 2 * snaps)
 
     def start_core(k):
         pltpu.make_async_remote_copy(
@@ -157,12 +176,20 @@
 
     load.wait()
     select(0)
-    pl.semaphore_wait(barrier, greeted)
+    pl.semaphore_wait(barrier, neighbours)
     start_core(0)
-    for k in range(1, n_chunk):
+    for level in range(levels - 1):
+        greet(near.at[level])
+        if level + 1 < n_chunk:
+            select(level + 1)
+            start_core(level + 1)
+        pl.semaphore_wait(near.at[level], neighbours)
+    start_rs(0)
+    for k in range(min(levels, n_chunk), n_chunk):
         select(k)
         start_core(k)
-        start_rs(k - 1)
+    for k in range(1, n_chunk - 1):
+        start_rs(k)
     pltpu.make_async_remote_copy(
         temps_ref.at[core], temps_ref.at[core], x_send, x_recv,
         device_id=partner, device_id_type=MESH,
@@ -194,11 +221,12 @@
     return pl.pallas_call(
         functools.partial(kernel, n_row, n_col, n_chunk, tiers),
         out_shape=pltpu.VMEM((rows_out, n_col * width), bf16),
-        in_specs=[pl.BlockSpec(memory_space=pl.ANY), pl.BlockSpec(memory_space=pltpu.VMEM)],
+        in_specs=[pl.BlockSpec(memory_space=pl.ANY)] * 2,
         out_specs=pl.BlockSpec(memory_space=pltpu.VMEM),
         scratch_shapes=[
             pltpu.VMEM((2, depth, width), bf16),
-            pltpu.VMEM((n_col, n_chunk, 2, rows_col // 2, tiers), jnp.int32),
+            pltpu.VMEM((tiers, sens), jnp.int32),
+            pltpu.VMEM((n_chunk, 2, n_col, rows_col // 2, tiers), jnp.int32),
             pltpu.VMEM((n_chunk, 2, 2, n_chip, SUB, depth // 2), bf16),
             pltpu.VMEM((n_chunk, 2, n_chip, SUB, depth // 2), bf16),
             pltpu.VMEM((n_chunk, 2, n_chip, SUB, depth // 2), bf16),
@@ -207,7 +235,9 @@
             pltpu.VMEM((n_chunk, n_col // 2 - 1, SUB, depth // 2), bf16),
             pltpu.VMEM((n_chunk, 2, n_chip, SUB, depth // 2), bf16),
             pltpu.VMEM((n_chunk, 2 * n_col, rows_col // 2, width), bf16),
-        ] + [pltpu.SemaphoreType.DMA((n_chunk,))] * 10 + [pltpu.SemaphoreType.DMA] * 3,
+        ] + [pltpu.SemaphoreType.DMA((n_chunk,))] * 10 + [pltpu.SemaphoreType.DMA] * 4 + [
+            pltpu.SemaphoreType.REGULAR((max(n_chip.bit_length(), n_col - 2) - 1,)),
+        ],
         compiler_params=pltpu.CompilerParams(collective_id=0, has_side_effects=True),
     )(temps.reshape(depth, width), sensors)
 

time: 31.9 us -> 31 us (0.972)
  Pallas kernels: 30.9 us -> 30.1 us
    pallas_call x1, Pallas kernels: 30.9 us -> 30.1 us  [body(): pl.pallas_call(functools.partial(kernel, n_row, n_col, n_chunk, tiers), o...]
where the time goes in v2:
time: 31 us; the launch traced here: 30.9 us
  Pallas kernels  30.1 us (97%)
  local copies, waits for them, and re-layouts  0.8 us (3%)
    pallas_call x1, Pallas kernels, body(): pl.pallas_call(functools.partial(kernel, n_row, n_col, n_chunk, tiers), o...  30.1 us
    unnamed x1, local copies, waits for them, and re-layouts  0.8 us

profile of v2, /device:TPU:0, one launch (start us, length us, event | category | flops | bytes accessed | tf_op | source)
XLA Modules:
  0.0 30.9 jit_solution(133304943398111800)
XLA Ops:
  0.0 30.1 %shard_map.28 = bf16[128,2048]{1,0:T(8,128)(2,1)S(1)} custom-call(bf16[768,512]{1,0:T(8,128)(2,1)} %bitcast.1, s32[12,512]{1,0:T(8,128)} %sens_hbm.1), custom_call_target="tpu_custom_call" | custom-call | tf_op jit(solution)/shard_map/pallas_call | solution.py:221
  30.1 0.8 %copy.4 = bf16[128,2048]{1,0:T(8,128)(2,1)} copy(bf16[128,2048]{1,0:T(8,128)(2,1)S(1)} %shard_map.28) | data formatting | bytes 1048576

commit v3 on v2

v3 whole, which is shorter than its diff:
```python
import functools

import jax
import numpy as np
import jax.numpy as jnp
from jax import lax
from jax.experimental import pallas as pl
from jax.experimental.pallas import tpu as pltpu
from jax.sharding import PartitionSpec as P

SUB = 8
PIECES = 8
FIRST = 5
EARLY = 2
UNITS = (2, 2, 2, 2)
Z_AG = 2.9
AG_OUT = 3.3
MESH = pl.DeviceIdType.MESH


def kernel(
    n_row, n_col, n_chunk, tiers,
    temps_hbm, sens_hbm, out_ref,
    temps_ref, sens_ref, sens_t, part, core_buf, pair_sum, rs_buf, z_src, z_buf, full, out_buf, ahead, ahead_buf, tally,
    c_send, c_recv, rs_send, rs_recv, z_send, z_recv,
    ag_send, ag_recv, o_send, o_recv, f_send, f_recv, g_send, g_recv, t_sem, s_sem, x_send, x_recv,
):
    r = lax.axis_index("row")
    z = lax.axis_index("col")
    core, chip = lax.rem(r, 2), r // 2
    other = 1 - core
    pair, parity = z // 2, lax.rem(z, 2)
    n_chip, n_pair = n_row // 2, n_col // 2
    depth, width = temps_ref.shape[1:]
    snaps, deep = depth // tiers, depth // 2
    rows_core = out_ref.shape[0] // 2
    half = rows_core // n_chunk
    first_unit = [sum(UNITS[:j]) for j in range(len(UNITS))]
    rows_half = n_chip * SUB
    n_half = n_col // 2
    side = z // n_half
    early = ahead.shape[2]
    mirror = n_col - 1 - z
    inner = (z == n_half - 1) | (z == n_half)
    slab = depth // PIECES
    scale = float(np.float32(1.0) / np.sqrt(np.float32(depth)))
    partner = (chip * 2 + other, z)

    bits = n_chip.bit_length() - 1
    cube = sorted(
        ((d, e) for d in range(n_chip) for e in range(2) if d or e),
        key=lambda peer: -peer[0].bit_count() - peer[1],
    )

    def flip(value, mask):
        for bit in range(bits):
            if mask >> bit & 1:
                value = value + (1 << bit) * (1 - 2 * lax.rem(value // (1 << bit), 2))
        return value

    def cube_peer(d, e):
        peer = flip(chip, d)
        side = lax.rem(parity + e, 2)
        return side, peer, (peer * 2 + core, pair * 2 + side)

    def far_peer(e):
        return lax.rem(z + 2 * e, n_col)

    load = pltpu.make_async_copy(temps_hbm, temps_ref.at[core], t_sem)
    load_sens = pltpu.make_async_copy(sens_hbm, sens_ref, s_sem)
    barrier = pltpu.get_barrier_semaphore()

    greeted = 0
    for d, e in cube:
        if d:
            pl.semaphore_signal(barrier, inc=1, device_id=cube_peer(d, e)[2], device_id_type=MESH)
            greeted += 1
    for h in range(2):
        for e in range(n_col):
            if h or e:
                device = (chip * 2 + lax.rem(core + h, 2), lax.rem(z + e, n_col))
                pl.semaphore_signal(barrier, inc=1, device_id=device, device_id_type=MESH)
                greeted += 1

    load_sens.start()
    load.start()

    first_pixel = (r * n_col + z) * width
    load_sens.wait()
    offsets = jnp.transpose(sens_ref[...] - first_pixel).reshape(n_col, 2, n_chunk, half, tiers)
    for k in range(n_chunk):
        for h in range(2):
            sens_t[k, h] = offsets[:, h, k]

    def wait_all(ref, sem):
        pltpu.make_async_copy(ref, ref, sem).wait()

    def units(j):
        return pl.ds(first_unit[j], UNITS[j])

    def select(j):
        rows = UNITS[j] * 2 * rows_half
        mine = sens_t[units(j)].reshape(rows, tiers)
        pixel_ids = lax.broadcasted_iota(jnp.int32, (rows, width), 1)
        for t in range(0, tiers, 2):
            two = []
            for u in (t, t + 1):
                hot = (pixel_ids == mine[:, u:u + 1]).astype(jnp.float32).astype(jnp.bfloat16)
                two.append(lax.dot_general(
                    hot, temps_ref[core, u * snaps:(u + 1) * snaps, :],
                    (((1,), (1,)), ((), ())), preferred_element_type=jnp.float32,
                ))
            both = jnp.concatenate(two, axis=1).astype(jnp.bfloat16)
            b, at = divmod(t * snaps, deep)
            part[units(j), :, b, :, :, at:at + 2 * snaps] = both.reshape(UNITS[j], 2, n_chip, SUB, 2 * snaps)

    def start_core(j):
        pltpu.make_async_remote_copy(
            part.at[units(j), other], core_buf.at[units(j)], c_send.at[j], c_recv.at[j],
            device_id=partner, device_id_type=MESH,
        ).start()

    def start_rs(j):
        k = units(j)
        wait_all(core_buf.at[k], c_recv.at[j])
        pair_sum[k] = part[k, core] + core_buf[k]
        for slot, (d, e) in enumerate(cube):
            member, peer, device = cube_peer(d, e)
            pltpu.make_async_remote_copy(
                pair_sum.at[k, member, peer], rs_buf.at[slot, k], rs_send.at[j], rs_recv.at[j],
                device_id=device, device_id_type=MESH,
            ).start()

    def start_z(j):
        k = units(j)
        wait_all(rs_buf.at[:, k], rs_recv.at[j])
        total = pair_sum[k, parity, chip]
        for slot in range(len(cube)):
            total = total + rs_buf[slot, k]
        z_src[k] = total
        for e in range(1, n_pair):
            pltpu.make_async_remote_copy(
                z_src.at[k], z_buf.at[e - 1, k], z_send.at[j], z_recv.at[j],
                device_id=(r, far_peer(e)), device_id_type=MESH,
            ).start()

    def start_ag(j):
        k = units(j)
        wait_all(z_buf.at[:, k], z_recv.at[j])
        total = z_src[k]
        for e in range(n_pair - 1):
            total = total + z_buf[e, k]
        full[k, parity, chip] = total
        for d, e in cube:
            mine = full.at[k, parity, chip]
            pltpu.make_async_remote_copy(
                mine, mine, ag_send.at[j], ag_recv.at[j], device_id=cube_peer(d, e)[2], device_id_type=MESH,
            ).start()

    def ahead_rows(batch):
        return pl.ds((0, FIRST * slab)[batch], (FIRST * slab, depth - FIRST * slab)[batch])

    def start_ahead(piece):
        batch = int(piece >= FIRST)
        rows = pl.ds(piece * slab, slab)

        @pl.when(inner)
        def _():
            pltpu.make_async_remote_copy(
                temps_ref.at[core, rows, pl.ds(0, early)], ahead.at[core, rows], f_send.at[batch], f_recv.at[batch],
                device_id=(r, mirror), device_id_type=MESH,
            ).start()

    def relay_ahead(batch):
        mine = ahead.at[core, ahead_rows(batch)]

        @pl.when(inner)
        def _():
            wait_all(mine, f_recv.at[batch])
            pltpu.make_async_remote_copy(
                mine, mine, g_send.at[batch], g_recv.at[batch], device_id=partner, device_id_type=MESH,
            ).start()

    def across(e):
        return jnp.where(side == 0, n_half + e, n_half - 1 - e)

    def beside(e):
        return side * n_half + lax.rem(z + e, n_half)

    def product(rows, weights):
        summed = jnp.dot(rows[0], weights[:deep, :], preferred_element_type=jnp.float32)
        summed += jnp.dot(rows[1], weights[deep:, :], preferred_element_type=jnp.float32)
        return (summed * scale).astype(jnp.bfloat16)

    def send_out(j, h, source, columns, peer):
        rows = pl.ds(pl.multiple_of(core * rows_core + first_unit[j] * half, half), UNITS[j] * half)
        pltpu.make_async_remote_copy(
            source, out_ref.at[rows, columns], o_send.at[j], o_recv.at[j],
            device_id=(chip * 2 + h, peer), device_id_type=MESH,
        ).start()

    def keep_out(j, source, columns):
        rows = pl.ds(pl.multiple_of(core * rows_core + first_unit[j] * half, half), UNITS[j] * half)
        out_ref[rows, columns] = source[...]

    def start_out(j):
        if j == 0:
            wait_all(temps_ref.at[other], x_recv)
        k = units(j)
        wait_all(rs_buf.at[:, k], ag_recv.at[j])
        rows = pl.ds(first_unit[j] * half, UNITS[j] * half)
        first = pl.multiple_of(z * width, width)
        readings = [full[k, b].reshape(UNITS[j] * rows_half, deep) for b in range(2)]
        for h in range(2):
            result = product(readings, temps_ref.at[h]).reshape(UNITS[j], n_col, half, width)
            for i in range(UNITS[j]):
                out_buf[h * n_col:(h + 1) * n_col, (first_unit[j] + i) * half:(first_unit[j] + i + 1) * half] = result[i]

        def send_beside():
            for e in range(1, n_half):
                for h in range(2):
                    send_out(j, h, out_buf.at[h * n_col + beside(e), rows], pl.ds(first, width), beside(e))

        @pl.when(inner)
        def _():
            for e in range(n_half):
                for h in range(2):
                    block = out_buf.at[h * n_col + across(e), rows, pl.ds(early, width - early)]
                    send_out(j, h, block, pl.ds(pl.multiple_of(first + early, 128), width - early), across(e))
            send_beside()

        @pl.when(jnp.logical_not(inner))
        def _():
            send_beside()
            for e in reversed(range(n_half)):
                for h in range(2):
                    send_out(j, h, out_buf.at[h * n_col + across(e), rows], pl.ds(first, width), across(e))

        send_out(j, other, out_buf.at[other * n_col + z, rows], pl.ds(first, width), z)
        keep_out(j, out_buf.at[core * n_col + z, rows], pl.ds(first, width))

    def start_near(j):
        @pl.when(inner)
        def _():
            if j == 0:
                for batch in range(2):
                    wait_all(ahead.at[other, ahead_rows(batch)], g_recv.at[batch])
            k = units(j)
            rows = pl.ds(first_unit[j] * half, UNITS[j] * half)
            columns = pl.ds(pl.multiple_of(mirror * width, width), early)
            readings = [full[k, b].reshape(UNITS[j], n_col, half, deep) for b in range(2)]
            readings = [
                jnp.where(side == 0, both[:, :n_half], both[:, n_half:]).reshape(UNITS[j] * n_half * half, deep)
                for both in readings
            ]
            for h in range(2):
                result = product(readings, ahead.at[h]).reshape(UNITS[j], n_half, half, early)
                for i in range(UNITS[j]):
                    ahead_buf[h * n_half:(h + 1) * n_half, (first_unit[j] + i) * half:(first_unit[j] + i + 1) * half] = result[i]
                for e in range(1, n_half):
                    member = lax.rem(z + e, n_half)
                    send_out(j, h, ahead_buf.at[h * n_half + member, rows], columns, side * n_half + member)
            member = lax.rem(z, n_half)
            send_out(j, other, ahead_buf.at[other * n_half + member, rows], columns, z)
            keep_out(j, ahead_buf.at[core * n_half + member, rows], columns)

    groups = len(UNITS)
    load.wait()
    select(0)
    pl.semaphore_wait(barrier, greeted)
    start_core(0)
    for piece in range(FIRST):
        start_ahead(piece)
    for j in range(1, groups):
        select(j)
        start_core(j)
        start_rs(j - 1)
    pltpu.make_async_remote_copy(
        temps_ref.at[core], temps_ref.at[core], x_send, x_recv,
        device_id=partner, device_id_type=MESH,
    ).start()
    start_rs(groups - 1)

    def rest_ahead(_):
        for piece in range(FIRST, PIECES):
            start_ahead(piece)

    due = []
    for j in range(groups):
        at = 0.53 * (first_unit[j] + UNITS[j])
        due += [(at, start_z, j), (at + Z_AG, start_ag, j), (at + Z_AG + AG_OUT, start_out, j)]
    last_z = 0.53 * n_chunk + 0.01
    due += [(last_z, rest_ahead, 0), (last_z + 0.1, relay_ahead, 0)]
    late = 0.53 * n_chunk + Z_AG + AG_OUT + 0.01
    due += [(late, relay_ahead, 1)]
    due += [(late + 0.02, start_near, j) for j in range(groups)]
    for _, stage, j in sorted(due, key=lambda item: item[0]):
        stage(j)
    wait_all(temps_ref.at[core], x_send)

    @pl.when(inner)
    def _():
        for batch in range(2):
            wait_all(ahead.at[core, ahead_rows(batch)], f_send.at[batch])
            wait_all(ahead.at[core, ahead_rows(batch)], g_send.at[batch])

    for j in range(groups):
        lanes = UNITS[j] * width // 128
        sent = (2 * n_col - 1) * lanes

        for sem in (o_recv, o_send):
            @pl.when(inner)
            def _():
                wait_all(tally.at[pl.ds(0, sent - UNITS[j] * early // 128)], sem.at[j])

            @pl.when(jnp.logical_not(inner))
            def _():
                wait_all(tally.at[pl.ds(0, sent)], sem.at[j])

        k = units(j)
        wait_all(core_buf.at[k], c_send.at[j])
        wait_all(rs_buf.at[:, k], rs_send.at[j])
        wait_all(z_buf.at[:, k], z_send.at[j])
        wait_all(rs_buf.at[:, k], ag_send.at[j])


def body(n_row, n_col, temps, sensors):
    tiers, snaps, width = temps.shape
    sens = sensors.shape[1]
    depth = tiers * snaps
    n_chunk = sens // (SUB * n_row)
    n_chip = n_row // 2
    rows_out = sens // n_col
    rows_core = rows_out // 2
    deep = depth // 2
    early = width * EARLY // 4 // 128 * 128
    bf16 = jnp.bfloat16
    return pl.pallas_call(
        functools.partial(kernel, n_row, n_col, n_chunk, tiers),
        out_shape=pltpu.VMEM((rows_out, n_col * width), bf16),
        in_specs=[pl.BlockSpec(memory_space=pl.ANY)] * 2,
        out_specs=pl.BlockSpec(memory_space=pltpu.VMEM),
        scratch_shapes=[
            pltpu.VMEM((2, depth, width), bf16),
            pltpu.VMEM((tiers, sens), jnp.int32),
            pltpu.VMEM((n_chunk, 2, n_col, rows_core // n_chunk, tiers), jnp.int32),
            pltpu.VMEM((n_chunk, 2, 2, n_chip, SUB, deep), bf16),
            pltpu.VMEM((n_chunk, 2, n_chip, SUB, deep), bf16),
            pltpu.VMEM((n_chunk, 2, n_chip, SUB, deep), bf16),
            pltpu.VMEM((2 * n_chip - 1, n_chunk, SUB, deep), bf16),
            pltpu.VMEM((n_chunk, SUB, deep), bf16),
            pltpu.VMEM((n_col // 2 - 1, n_chunk, SUB, deep), bf16),
            pltpu.VMEM((n_chunk, 2, n_chip, SUB, deep), bf16),
            pltpu.VMEM((2 * n_col, rows_core, width), bf16),
            pltpu.VMEM((2, depth, early), bf16),
            pltpu.VMEM((n_col, rows_core, early), bf16),
            pltpu.VMEM((2 * n_col * max(UNITS) * width // 128, rows_core // n_chunk, 128), bf16),
        ] + [pltpu.SemaphoreType.DMA((len(UNITS),))] * 10
        + [pltpu.SemaphoreType.DMA((2,))] * 4 + [pltpu.SemaphoreType.DMA] * 4,
        compiler_params=pltpu.CompilerParams(collective_id=0, has_side_effects=True),
    )(temps.reshape(depth, width), sensors)


def solution(mesh):
    placed = (P(None, None, ("row", "col")), P())
    return jax.shard_map(
        functools.partial(body, mesh.shape["row"], mesh.shape["col"]),
        mesh=mesh, in_specs=placed, out_specs=P("col", "row"), check_vma=False,
    )
```

time: 31 us -> 29.9 us (0.965)
  Pallas kernels: 30.1 us -> 29 us
    pallas_call x1, Pallas kernels: 30.1 us -> 29 us  [body(): pl.pallas_call(functools.partial(kernel, n_row, n_col, n_chunk, tiers), o...]
where the time goes in v3:
time: 29.9 us; the launch traced here: 29.8 us
  Pallas kernels  29 us (97%)
  local copies, waits for them, and re-layouts  0.8 us (3%)
    pallas_call x1, Pallas kernels, body(): pl.pallas_call(functools.partial(kernel, n_row, n_col, n_chunk, tiers), o...  29 us
    unnamed x1, local copies, waits for them, and re-layouts  0.8 us

profile of v3, /device:TPU:0, one launch (start us, length us, event | category | flops | bytes accessed | tf_op | source)
XLA Modules:
  0.0 29.8 jit_solution(13725247287016285476)
XLA Ops:
  0.0 29.0 %shard_map.28 = bf16[128,2048]{1,0:T(8,128)(2,1)S(1)} custom-call(bf16[768,512]{1,0:T(8,128)(2,1)} %bitcast.1, s32[12,512]{1,0:T(8,128)} %sens_hbm.1), custom_call_target="tpu_custom_call" | custom-call | tf_op jit(solution)/shard_map/pallas_call | solution.py:338
  29.0 0.8 %copy.4 = bf16[128,2048]{1,0:T(8,128)(2,1)} copy(bf16[128,2048]{1,0:T(8,128)(2,1)S(1)} %shard_map.28) | data formatting | bytes 1048576

commit v4 on v3

--- a/solution.py
+++ b/solution.py
@@ -9,8 +9,8 @@
 from jax.sharding import PartitionSpec as P
 
 SUB = 8
-PIECES = 8
-FIRST = 5
+PIECES = 16
+FIRST = 10
 EARLY = 2
 UNITS = (2, 2, 2, 2)
 Z_AG = 2.9
@@ -231,10 +231,13 @@
 
         @pl.when(jnp.logical_not(inner))
         def _():
-            send_beside()
+            if j < len(UNITS) - 1:
+                send_beside()
             for e in reversed(range(n_half)):
                 for h in range(2):
                     send_out(j, h, out_buf.at[h * n_col + across(e), rows], pl.ds(first, width), across(e))
+            if j == len(UNITS) - 1:
+                send_beside()
 
         send_out(j, other, out_buf.at[other * n_col + z, rows], pl.ds(first, width), z)
         keep_out(j, out_buf.at[core * n_col + z, rows], pl.ds(first, width))
@@ -274,25 +277,32 @@
     for j in range(1, groups):
         select(j)
         start_core(j)
-        start_rs(j - 1)
+        if j == 1:
+            pl.when(core == 1)(functools.partial(start_rs, 0))
+        elif j == 2:
+            pl.when(core == 0)(functools.partial(start_rs, 0))
+            start_rs(1)
+        else:
+            start_rs(j - 1)
     pltpu.make_async_remote_copy(
         temps_ref.at[core], temps_ref.at[core], x_send, x_recv,
         device_id=partner, device_id_type=MESH,
     ).start()
     start_rs(groups - 1)
 
-    def rest_ahead(_):
-        for piece in range(FIRST, PIECES):
+    def start_z_ahead(j):
+        start_z(j)
+        for piece in range(FIRST + j, FIRST + j + 1 if j < groups - 1 else PIECES):
             start_ahead(piece)
 
     due = []
     for j in range(groups):
         at = 0.53 * (first_unit[j] + UNITS[j])
-        due += [(at, start_z, j), (at + Z_AG, start_ag, j), (at + Z_AG + AG_OUT, start_out, j)]
+        due += [(at, start_z_ahead, j), (at + Z_AG, start_ag, j), (at + Z_AG + AG_OUT, start_out, j)]
     last_z = 0.53 * n_chunk + 0.01
-    due += [(last_z, rest_ahead, 0), (last_z + 0.1, relay_ahead, 0)]
+    due += [(last_z + 0.1, relay_ahead, 0)]
     late = 0.53 * n_chunk + Z_AG + AG_OUT + 0.01
-    due += [(late, relay_ahead, 1)]
+    due += [(late - 0.02, relay_ahead, 1)]
     due += [(late + 0.02, start_near, j) for j in range(groups)]
     for _, stage, j in sorted(due, key=lambda item: item[0]):
         stage(j)

time: 29.9 us -> 29.9 us (level)
  no operation moved by 1% of the time
where the time goes in v4:
time: 29.9 us; the launch traced here: 29.7 us
  Pallas kernels  28.9 us (97%)
  local copies, waits for them, and re-layouts  0.8 us (3%)
    pallas_call x1, Pallas kernels, body(): pl.pallas_call(functools.partial(kernel, n_row, n_col, n_chunk, tiers), o...  28.9 us
    unnamed x1, local copies, waits for them, and re-layouts  0.8 us

profile of v4, /device:TPU:0, one launch (start us, length us, event | category | flops | bytes accessed | tf_op | source)
XLA Modules:
  0.0 29.7 jit_solution(3104847848753543059)
XLA Ops:
  0.0 28.9 %shard_map.28 = bf16[128,2048]{1,0:T(8,128)(2,1)S(1)} custom-call(bf16[768,512]{1,0:T(8,128)(2,1)} %bitcast.1, s32[12,512]{1,0:T(8,128)} %sens_hbm.1), custom_call_target="tpu_custom_call" | custom-call | tf_op jit(solution)/shard_map/pallas_call | solution.py:348
  28.9 0.8 %copy.4 = bf16[128,2048]{1,0:T(8,128)(2,1)} copy(bf16[128,2048]{1,0:T(8,128)(2,1)S(1)} %shard_map.28) | data formatting | bytes 1048576
